TPU v7x, 512 devices: a whole 4x8x8 slice. The times are simulated.
512 devices in a mesh: row: 16 (over z, core), col: 4 (over x), depth: 8 (over y).
Axes of the slice: x: 4, y: 8, z: 8, core: 2. Of those that a mesh axis runs over, the one named last changes fastest.
Arguments:
- intersection_re: bfloat16 [8, 4096, 4096], P('depth', ('row', 'col')), may hold values from -1 to 1, as said below
- intersection_im: bfloat16 [8, 4096, 4096], P('depth', ('row', 'col')), may hold values from -1 to 1, as said below
- weights: float32 [8], replicated, may hold values from 0.5 to 2
- shells: int32 [8, 3], replicated, may hold values from -2 to 2
- rotation: bfloat16 [4096, 4096], P(('row', 'col')), may hold values from -6 to 6
Outputs:
- updated: float32 [4096, 4096], P(('row', 'col'), 'depth')
Inputs may be any that keep to these rules, and one draw needn't show every extreme that they name: `intersection_re`: diagonal entries lie in 0.5 to 1. `intersection_im`: diagonal entries lie in -0.6 to 0.6.
All inputs are finite; a program needn't handle non-finite values.
Results may differ from a plain program's by a relative error of at most 0.035.
Values may be sent and summed in bfloat16 or wider, within the bound.
No kernel may reach another device: no remote copies, remote signals or barrier semaphores. Data moves between devices by JAX's collectives and lax.ppermute only.
A program may use at most 64 MiB of HBM per device.

v0:
```python
import math
import jax
import jax.numpy as jnp
from jax import lax
from jax.sharding import PartitionSpec as P

TERMS = 8
LATTICE = 0.25


def from_everyone(shard, axis):
    copies = jnp.broadcast_to(shard, (lax.axis_size(axis), *shard.shape))
    return lax.all_to_all(copies, axis, split_axis=0, concat_axis=0, tiled=True)


def in_order(parts, dim):
    dims = list(parts.shape[1:])
    dims[dim] *= parts.shape[0]
    return jnp.moveaxis(parts, 0, dim).reshape(dims)


def gather_directly(shard, axis, dim):
    parts = from_everyone(shard, axis)
    return in_order(parts, dim)


def over_copies(shard, axis):
    everything = from_everyone(shard, axis)
    return jnp.sum(everything, axis=0)


def cut_along(shard, dim, devices):
    before, after = (shard.shape[:dim], shard.shape[dim + 1 :])
    return jnp.moveaxis(shard.reshape(*before, devices, -1, *after), dim, 0)


def sum_at_owner(shard, axis, dim):
    parts = cut_along(shard, dim, lax.axis_size(axis))
    arrived = lax.all_to_all(parts, axis, split_axis=0, concat_axis=0, tiled=True)
    return arrived.sum(axis=0)


def per_device(intersection_re, intersection_im, weights, shells, rotation):
    shells_here = intersection_re.shape[0]
    slab_rows = intersection_re.shape[1]
    width = intersection_re.shape[2]
    position = lax.axis_index(("row", "col"))
    layer_index = lax.axis_index("depth")
    depth_count = lax.axis_size("depth")
    block_re = lax.dynamic_slice_in_dim(intersection_re, position * slab_rows, slab_rows, 2)
    block_im = lax.dynamic_slice_in_dim(intersection_im, position * slab_rows, slab_rows, 2)
    diag_piece = jnp.stack(
        [jnp.diagonal(block_re, axis1=1, axis2=2), jnp.diagonal(block_im, axis1=1, axis2=2)], 1
    )
    first_shell = layer_index * shells_here
    own_weights = lax.dynamic_slice_in_dim(weights, first_shell, shells_here, 0)
    own_vectors = (
        lax.dynamic_slice_in_dim(shells, first_shell, shells_here, 0).astype(jnp.float32) * LATTICE
    )
    diagonals = gather_directly(diag_piece, ("row", "col"), 2).astype(jnp.float32)
    diag_re = diagonals[:, 0]
    diag_im = diagonals[:, 1]
    phase_own = jnp.arctan2(diag_im, diag_re)
    partial_centre = -jnp.einsum("bk,bn->kn", own_weights[:, None] * own_vectors, phase_own)
    centre = over_copies(partial_centre, "depth")
    spread = phase_own + jnp.einsum("bk,kn->bn", own_vectors, centre)
    modulus = diag_re * diag_re + diag_im * diag_im
    values_re = intersection_re.astype(jnp.float32)
    values_im = intersection_im.astype(jnp.float32)
    terms = values_re * diag_re[:, None, :] + values_im * diag_im[:, None, :]
    terms = (
        terms
        - spread[:, None, :]
        * (values_im * diag_re[:, None, :] - values_re * diag_im[:, None, :])
        / modulus[:, None, :]
    )
    local_sum = jnp.sum(own_weights[:, None, None] * terms, 0)
    factor = 1.25 / math.sqrt(depth_count * shells_here)
    slab_cols = width // depth_count
    mirrored = lax.all_to_all(local_sum, ("row", "col"), split_axis=1, concat_axis=0, tiled=True).T
    operator_rows = sum_at_owner(local_sum - mirrored, "depth", 1) * factor
    operator_piece = operator_rows.astype(jnp.bfloat16)
    operator_cols = lax.all_gather(operator_piece, ("row", "col"), axis=0, tiled=True)
    accum = lax.dynamic_slice_in_dim(rotation, layer_index * slab_cols, slab_cols, 1).astype(
        jnp.float32
    )
    product = jnp.dot(rotation, operator_cols, preferred_element_type=jnp.float32)
    for order in range(1, TERMS):
        series_term = (product / order).astype(jnp.bfloat16)
        accum = accum + series_term.astype(jnp.float32)
        if order + 1 < TERMS:
            piece = gather_directly(series_term, "depth", 1)
            matching = lax.slice_in_dim(operator_cols, 0, piece.shape[1], axis=0)
            product = jnp.zeros_like(accum) + jnp.dot(
                piece, matching, preferred_element_type=jnp.float32
            )
    return accum


def solution(mesh):
    in_specs = (
        P("depth", ("row", "col"), None),
        P("depth", ("row", "col"), None),
        P(),
        P(),
        P(("row", "col"), None),
    )
    out_specs = P(("row", "col"), "depth")
    return jax.shard_map(
        per_device, mesh=mesh, in_specs=in_specs, out_specs=out_specs, check_vma=False
    )
```

profile of v0, /device:TPU:8, one launch (start us, length us, event | category | flops | bytes accessed | tf_op | source)
XLA Modules:
  0.0 354.2 jit_solution(16714782614347129712)
XLA Ops:
  6.5 0.0 copy-start.3
  6.5 0.0 copy-start.2
  6.6 0.9 dynamic-slice_bitcast_fusion
  7.5 0.9 gather_fusion.1
  8.3 0.9 gather_fusion
  9.2 0.6 broadcast_in_dim.34
  9.9 13.8 %all-to-all-start = ((bf16[64,1,2,64]{3,2,1,0:T(2,128)(2,1)}), bf16[64,1,2,64]{3,2,1,0:T(2,128)(2,1)S(1)}, u32[]{:S(2)}, u32[]{:S(2)}) async-start(bf16[64,1,2,64]{3,2,1,0:T(2,128)(2,1)} %broadcast_in_dim.34), calls=%async_computation | async-start | bytes 65536 | tf_op jit(solution)/shard_map/all_to_all | solution.py:13
  23.7 0.0 all-gather.2.cloned.1.call-start
  23.7 1.3 dynamic_slice.16
  25.7 0.9 multiply_reduce_fusion.1
  26.6 6.6 %all-to-all-done = bf16[64,1,2,64]{3,2,1,0:T(2,128)(2,1)S(1)} async-done(((bf16[64,1,2,64]{3,2,1,0:T(2,128)(2,1)}), bf16[64,1,2,64]{3,2,1,0:T(2,128)(2,1)S(1)}, u32[]{:S(2)}, u32[]{:S(2)}) %all-to-all-start) | async-done | bytes 16416 | tf_op jit(solution)/shard_map/all_to_all | solution.py:13
  33.3 0.1 reshape.91
  33.4 0.2 fusion.17
  33.7 0.1 multiply_negate_fusion
  33.7 0.1 broadcast_in_dim.35
  33.8 23.1 %all_to_all.64 = f32[8,3,4096]{2,1,0:T(4,128)S(1)} all-to-all(f32[8,3,4096]{2,1,0:T(4,128)S(1)} %broadcast_in_dim.35), channel_id=1, replica_groups=mesh['row'=16,'col'=4,'depth'=8] {'depth'}, dimensions={0} | all-to-all | bytes 786432 | tf_op jit(solution)/shard_map/all_to_all | solution.py:13
  56.9 0.1 reduce_sum.24
  57.0 0.1 fusion.15
  57.2 0.0 copy-done.3
  57.2 0.0 copy-done.2
  57.2 1.1 fusion.11
  58.3 2.2 all_to_all.43
  60.5 2.8 copy.56
  63.3 2.3 reshape.115
  65.6 33.6 %all_to_all.65 = f32[64,1,4096]{2,1,0:T(1,128)S(1)} all-to-all(f32[64,1,4096]{2,1,0:T(1,128)} %reshape.115), channel_id=1, replica_groups=mesh['row'=16,'col'=4,'depth'=8] {'row','col'}, dimensions={0} | all-to-all | bytes 2097152 | tf_op jit(solution)/shard_map/all_to_all | solution.py:80
  99.2 0.5 broadcast.60
  99.7 4.5 %reduce.4 = f32[64,4096]{1,0:T(8,128)} reduce(f32[64,1,4096]{2,1,0:T(1,128)S(1)} %all_to_all.65, f32[]{:T(128)} %broadcast.60), dimensions={1}, to_apply=%all_to_all.44.reduce_sub_computation | reduce | bytes 2097156 | tf_op jit(solution)/shard_map/all_to_all | solution.py:80
  104.2 2.0 reshape.116
  106.2 1.6 copy.39
  107.8 1.3 bitcast_subtract_fusion
  109.1 0.0 copy-start.1
  109.1 0.6 copy.54
  109.7 0.6 copy.40
  110.4 30.6 %all_to_all.66 = f32[8,64,512]{2,1,0:T(8,128)S(1)} all-to-all(f32[8,64,512]{2,1,0:T(8,128)S(1)} %copy.40), channel_id=1, replica_groups=mesh['row'=16,'col'=4,'depth'=8] {'depth'}, dimensions={0} | all-to-all | bytes 2097152 | tf_op jit(solution)/shard_map/all_to_all | solution.py:39
  140.9 0.1 reduce_sum.26
  141.0 0.6 multiply_convert_fusion
  141.7 0.0 all-gather.2.cloned.1.call-update
  141.7 78.4 %all-gather.2.cloned.1.call-done = bf16[4096,512]{1,0:T(8,128)(2,1)} async-done(((bf16[64,512]{1,0:T(8,128)(2,1)}), bf16[4096,512]{1,0:T(8,128)(2,1)}) %all-gather.2.cloned.1.call-update) | async-done | bytes 4194320 | tf_op jit(solution)/shard_map/all_gather | solution.py:83
  220.1 0.0 copy-done.1
  220.1 0.0 copy-start
  220.1 3.2 fusion.8
  223.3 23.5 %all_to_all.67 = bf16[8,64,512]{2,1,0:T(8,128)(2,1)S(1)} all-to-all(bf16[8,64,512]{2,1,0:T(8,128)(2,1)S(1)} %broadcast_in_dim.36), channel_id=1, replica_groups=mesh['row'=16,'col'=4,'depth'=8] {'depth'}, dimensions={0} | all-to-all | bytes 1048576 | tf_op jit(solution)/shard_map/all_to_all | solution.py:13
  246.9 0.0 copy-done
  246.9 0.8 fusion
  247.8 19.7 %all_to_all.68 = bf16[8,64,512]{2,1,0:T(8,128)(2,1)S(1)} all-to-all(bf16[8,64,512]{2,1,0:T(8,128)(2,1)S(1)} %broadcast_in_dim.37), channel_id=1, replica_groups=mesh['row'=16,'col'=4,'depth'=8] {'depth'}, dimensions={0} | all-to-all | bytes 1048576 | tf_op jit(solution)/shard_map/all_to_all | solution.py:13
  267.6 0.8 fusion.1
  268.5 18.5 %all_to_all.69 = bf16[8,64,512]{2,1,0:T(8,128)(2,1)S(1)} all-to-all(bf16[8,64,512]{2,1,0:T(8,128)(2,1)S(1)} %broadcast_in_dim.38), channel_id=1, replica_groups=mesh['row'=16,'col'=4,'depth'=8] {'depth'}, dimensions={0} | all-to-all | bytes 1048576 | tf_op jit(solution)/shard_map/all_to_all | solution.py:13
  287.0 0.8 fusion.2
  287.9 17.6 %all_to_all.70 = bf16[8,64,512]{2,1,0:T(8,128)(2,1)S(1)} all-to-all(bf16[8,64,512]{2,1,0:T(8,128)(2,1)S(1)} %broadcast_in_dim.39), channel_id=1, replica_groups=mesh['row'=16,'col'=4,'depth'=8] {'depth'}, dimensions={0} | all-to-all | bytes 1048576 | tf_op jit(solution)/shard_map/all_to_all | solution.py:13
  305.6 0.8 fusion.3
  306.5 17.6 %all_to_all.71 = bf16[8,64,512]{2,1,0:T(8,128)(2,1)S(1)} all-to-all(bf16[8,64,512]{2,1,0:T(8,128)(2,1)S(1)} %broadcast_in_dim.40), channel_id=1, replica_groups=mesh['row'=16,'col'=4,'depth'=8] {'depth'}, dimensions={0} | all-to-all | bytes 1048576 | tf_op jit(solution)/shard_map/all_to_all | solution.py:13
  324.2 0.8 fusion.4
  325.0 0.8 broadcast_in_dim.41
  325.8 4.9 %all-to-all-start.9 = ((bf16[8,64,512]{2,1,0:T(8,128)(2,1)}), bf16[8,64,512]{2,1,0:T(8,128)(2,1)S(1)}, u32[]{:S(2)}, u32[]{:S(2)}) async-start(bf16[8,64,512]{2,1,0:T(8,128)(2,1)} %broadcast_in_dim.41), calls=%async_computation.9 | async-start | bytes 1048576 | tf_op jit(solution)/shard_map/all_to_all | solution.py:13
  330.7 13.0 %all-to-all-done.9 = bf16[8,64,512]{2,1,0:T(8,128)(2,1)S(1)} async-done(((bf16[8,64,512]{2,1,0:T(8,128)(2,1)}), bf16[8,64,512]{2,1,0:T(8,128)(2,1)S(1)}, u32[]{:S(2)}, u32[]{:S(2)}) %all-to-all-start.9) | async-done | bytes 524320 | tf_op jit(solution)/shard_map/all_to_all | solution.py:13
  343.7 3.7 %fusion.7 = f32[64,512]{1,0:T(8,128)} fusion(bf16[64,4096]{1,0:T(8,128)(2,1)S(1)} %bitcast.88, bf16[4096,512]{1,0:T(8,128)(2,1)} %all-gather.2.cloned.1.call-done, bf16[64,512]{1,0:T(8,128)(2,1)S(1)} %fusion.4, bf16[64,512]{1,0:T(8,128)(2,1)S(1)} %fusion.3, bf16[64,512]{1,0:T(8,128)(2,1)S(1)} %fusion.2, bf16[64,512]{1,0:T(8,128)(2,1)S(1)} %fusion.1, ...), kind=kOutput, calls=%fused_computation.19 | convolution fusion | flops 268992512 | bytes 5308420 | tf_op jit(solution)/shard_map/dot_general | solution.py:94
  (16 shorter events, 0.5 us)
Async XLA Ops:
  6.5 50.7 %copy-start.3 = (bf16[1,64,4096]{2,1,0:T(8,128)(2,1)S(1)}, bf16[1,64,4096]{2,1,0:T(8,128)(2,1)}, u32[]{:S(2)}) copy-start(bf16[1,64,4096]{2,1,0:T(8,128)(2,1)} %param.6) | copy-start | bytes 1572868
  6.5 50.7 %copy-start.2 = (bf16[1,64,4096]{2,1,0:T(8,128)(2,1)S(1)}, bf16[1,64,4096]{2,1,0:T(8,128)(2,1)}, u32[]{:S(2)}) copy-start(bf16[1,64,4096]{2,1,0:T(8,128)(2,1)} %param.5) | copy-start | bytes 1572868
  9.9 23.4 %all-to-all-start = ((bf16[64,1,2,64]{3,2,1,0:T(2,128)(2,1)}), bf16[64,1,2,64]{3,2,1,0:T(2,128)(2,1)S(1)}, u32[]{:S(2)}, u32[]{:S(2)}) async-start(bf16[64,1,2,64]{3,2,1,0:T(2,128)(2,1)} %broadcast_in_dim.34), calls=%async_computation | async-start | bytes 65536 | tf_op jit(solution)/shard_map/all_to_all | solution.py:13
  23.7 196.4 %all-gather.2.cloned.1.call-start = ((), (), s32[]{:S(2)}) async-start(), calls=%async_computation.10 | async-start | bytes 4259840 | tf_op jit(solution)/shard_map/all_gather | solution.py:83
  109.1 111.0 %copy-start.1 = (bf16[64,4096]{1,0:T(8,128)(2,1)S(1)}, bf16[64,4096]{1,0:T(8,128)(2,1)}, u32[]{:S(2)}) copy-start(bf16[64,4096]{1,0:T(8,128)(2,1)} %param.9) | copy-start | bytes 1572868
  220.1 26.8 %copy-start = (bf16[4096,512]{1,0:T(8,128)(2,1)S(1)}, bf16[4096,512]{1,0:T(8,128)(2,1)}, u32[]{:S(2)}) copy-start(bf16[4096,512]{1,0:T(8,128)(2,1)} %all-gather.2.cloned.1.call-done) | copy-start | bytes 12582916
  325.8 17.8 %all-to-all-start.9 = ((bf16[8,64,512]{2,1,0:T(8,128)(2,1)}), bf16[8,64,512]{2,1,0:T(8,128)(2,1)S(1)}, u32[]{:S(2)}, u32[]{:S(2)}) async-start(bf16[8,64,512]{2,1,0:T(8,128)(2,1)} %broadcast_in_dim.41), calls=%async_computation.9 | async-start | bytes 1048576 | tf_op jit(solution)/shard_map/all_to_all | solution.py:13
Sparse Core Ops, SparseCore 0:
  141.8 78.2 all-gather.1
where the time goes:
time: 355 us; the launch traced here: 354 us
  blocking collectives  184 us (52%)
  waiting for transfers between devices  98 us (28%)
  local copies, waits for them, and re-layouts  18.7 us (5%)
  starting transfers between devices  18.7 us (5%)
  between operations  14.4 us (4%)
  matrix products  11.2 us (3%)
  other arithmetic  9.01 us (3%)
    all_to_all x6, blocking collectives, from_everyone(): return lax.all_to_all(copies, axis, split_axis=0, concat_axis=0, tiled=True)  120 us
    all_gather x1, waiting for transfers between devices, per_device(): lax.all_gather(operator_piece, ('row', 'col'), axis=0, tiled=True)  78.4 us
    all_to_all x1, blocking collectives, per_device(): lax.all_to_all(local_sum, ('row', 'col'), split_axis=1, concat_axis=0, ti...  33.6 us
    all_to_all x1, blocking collectives, sum_at_owner(): lax.all_to_all(parts, axis, split_axis=0, concat_axis=0, tiled=True)  30.6 us
    all_to_all x2, waiting for transfers between devices, from_everyone(): return lax.all_to_all(copies, axis, split_axis=0, concat_axis=0, tiled=True)  19.6 us
    all_to_all x2, starting transfers between devices, from_everyone(): return lax.all_to_all(copies, axis, split_axis=0, concat_axis=0, tiled=True)  18.6 us
    dot_general x6, matrix products, per_device(): jnp.dot(piece, matching, preferred_element_type=jnp.float32)  7.87 us
  transfers between devices with their start and end apart: 3, of which 3 were waited for; matrix products, arithmetic and copies ran while one was open for 1% of the time, Pallas kernels for 0%

commit v1 on v0

--- a/solution.py
+++ b/solution.py
@@ -6,6 +6,26 @@
 
 TERMS = 8
 LATTICE = 0.25
+
+
+def tracks_post(xin, at_axis):
+    f_now = list(xin.shape[1:])
+    f_now[at_axis] *= xin.shape[0]
+    return jnp.moveaxis(xin, 0, at_axis).reshape(f_now)
+
+
+def _switch_task(v0, mesh_dim):
+    amount_of = lax.psum(1, mesh_dim)
+    response = v0[None]
+    for q in range(amount_of.bit_length() - 1):
+        u1 = 1 << q
+        arr_now = lax.ppermute(
+            response, mesh_dim, tuple(((j0, j0 ^ u1) for j0 in range(amount_of)))
+        )
+        outcome_arr = jnp.stack([response, arr_now])
+        reply = lax.axis_index(mesh_dim) >> q & 1
+        response = jnp.where(reply == 0, outcome_arr, outcome_arr[::-1]).reshape(-1, *v0.shape)
+    return response
 
 
 def from_everyone(shard, axis):
@@ -80,7 +100,11 @@
     mirrored = lax.all_to_all(local_sum, ("row", "col"), split_axis=1, concat_axis=0, tiled=True).T
     operator_rows = sum_at_owner(local_sum - mirrored, "depth", 1) * factor
     operator_piece = operator_rows.astype(jnp.bfloat16)
-    operator_cols = lax.all_gather(operator_piece, ("row", "col"), axis=0, tiled=True)
+
+    def unite_cells(d_out, my_tile, view):
+        return tracks_post(_switch_task(my_tile, view), d_out)
+
+    operator_cols = unite_cells(0, operator_piece, ("row", "col"))
     accum = lax.dynamic_slice_in_dim(rotation, layer_index * slab_cols, slab_cols, 1).astype(
         jnp.float32
     )

time: 355 us -> 444 us (1.25)
  the two profiles are of different devices: /device:TPU:8 before, /device:TPU:2 now
where the time goes in v1:
time: 444 us; the launch traced here: 443 us
  blocking collectives  184 us (41%)
  waiting for transfers between devices  179 us (40%)
  starting transfers between devices  38.4 us (9%)
  local copies, waits for them, and re-layouts  18.5 us (4%)
  other arithmetic  12.8 us (3%)
  matrix products  8.84 us (2%)
    ppermute x6, waiting for transfers between devices, _switch_task(): lax.ppermute(response, mesh_dim, tuple(((j0, j0 ^ u1) for j0 in range(amo...  159 us
    all_to_all x6, blocking collectives, from_everyone(): return lax.all_to_all(copies, axis, split_axis=0, concat_axis=0, tiled=True)  120 us
    all_to_all x1, blocking collectives, per_device(): lax.all_to_all(local_sum, ('row', 'col'), split_axis=1, concat_axis=0, ti...  34.5 us
    all_to_all x1, blocking collectives, sum_at_owner(): lax.all_to_all(parts, axis, split_axis=0, concat_axis=0, tiled=True)  30.1 us
    ppermute x6, starting transfers between devices, _switch_task(): lax.ppermute(response, mesh_dim, tuple(((j0, j0 ^ u1) for j0 in range(amo...  21.1 us
    all_to_all x2, waiting for transfers between devices, from_everyone(): return lax.all_to_all(copies, axis, split_axis=0, concat_axis=0, tiled=True)  20.1 us
    all_to_all x2, starting transfers between devices, from_everyone(): return lax.all_to_all(copies, axis, split_axis=0, concat_axis=0, tiled=True)  17.4 us
  transfers between devices with their start and end apart: 8, of which 8 were waited for; matrix products, arithmetic and copies ran while one was open for 0% of the time, Pallas kernels for 0%

profile of v1, /device:TPU:2, one launch (start us, length us, event | category | flops | bytes accessed | tf_op | source)
XLA Modules:
  0.0 443.4 jit_solution(11822035221695719354)
XLA Ops:
  0.0 0.9 dynamic-slice_bitcast_fusion
  0.9 0.9 gather_fusion.1
  1.8 0.9 gather_fusion
  2.7 0.6 broadcast_in_dim.35
  3.3 13.9 %all-to-all-start = ((bf16[64,1,2,64]{3,2,1,0:T(2,128)(2,1)}), bf16[64,1,2,64]{3,2,1,0:T(2,128)(2,1)S(1)}, u32[]{:S(2)}, u32[]{:S(2)}) async-start(bf16[64,1,2,64]{3,2,1,0:T(2,128)(2,1)} %broadcast_in_dim.35), calls=%async_computation | async-start | bytes 65536 | tf_op jit(solution)/shard_map/all_to_all | solution.py:33
  17.2 1.3 dynamic_slice.16
  19.1 0.9 multiply_reduce_fusion.1
  20.0 5.8 %all-to-all-done = bf16[64,1,2,64]{3,2,1,0:T(2,128)(2,1)S(1)} async-done(((bf16[64,1,2,64]{3,2,1,0:T(2,128)(2,1)}), bf16[64,1,2,64]{3,2,1,0:T(2,128)(2,1)S(1)}, u32[]{:S(2)}, u32[]{:S(2)}) %all-to-all-start) | async-done | bytes 16416 | tf_op jit(solution)/shard_map/all_to_all | solution.py:33
  25.8 0.1 reshape.137
  25.9 0.2 fusion.21
  26.2 0.1 multiply_negate_fusion
  26.3 0.1 broadcast_in_dim.36
  26.3 24.1 %all_to_all.64 = f32[8,3,4096]{2,1,0:T(4,128)S(1)} all-to-all(f32[8,3,4096]{2,1,0:T(4,128)S(1)} %broadcast_in_dim.36), channel_id=1, replica_groups=mesh['row'=16,'col'=4,'depth'=8] {'depth'}, dimensions={0} | all-to-all | bytes 786432 | tf_op jit(solution)/shard_map/all_to_all | solution.py:33
  50.5 0.1 reduce_sum.24
  50.6 0.1 fusion.19
  50.8 1.0 fusion.11
  51.8 2.2 all_to_all.43
  54.0 2.8 copy.62
  56.8 2.3 reshape.161
  59.1 34.5 %all_to_all.65 = f32[64,1,4096]{2,1,0:T(1,128)S(1)} all-to-all(f32[64,1,4096]{2,1,0:T(1,128)} %reshape.161), channel_id=1, replica_groups=mesh['row'=16,'col'=4,'depth'=8] {'row','col'}, dimensions={0} | all-to-all | bytes 2097152 | tf_op jit(solution)/shard_map/all_to_all | solution.py:100
  93.6 0.5 broadcast.78
  94.1 4.4 reduce.4
  98.5 2.0 reshape.162
  100.5 1.6 copy.44
  102.1 1.3 bitcast_subtract_fusion
  103.4 0.6 copy.60
  104.0 0.6 copy.45
  104.6 30.1 %all_to_all.66 = f32[8,64,512]{2,1,0:T(8,128)S(1)} all-to-all(f32[8,64,512]{2,1,0:T(8,128)S(1)} %copy.45), channel_id=1, replica_groups=mesh['row'=16,'col'=4,'depth'=8] {'depth'}, dimensions={0} | all-to-all | bytes 2097152 | tf_op jit(solution)/shard_map/all_to_all | solution.py:59
  134.7 0.1 reduce_sum.26
  134.8 3.0 collective-permute-start
  137.8 3.2 collective-permute-done
  141.0 4.2 collective-permute-start.1
  145.3 4.1 collective-permute-done.1
  149.5 1.9 collective-permute-start.2
  151.4 1.5 collective-permute-done.2
  152.9 0.1 pad_maximum_fusion.3
  153.0 0.1 reverse_select_fusion.3
  153.1 3.6 collective-permute-start.3
  156.6 12.3 %collective-permute-done.3 = bf16[8,64,512]{2,1,0:T(8,128)(2,1)S(1)} collective-permute-done((bf16[8,64,512]{2,1,0:T(8,128)(2,1)S(1)}, bf16[8,64,512]{2,1,0:T(8,128)(2,1)S(1)}, u32[]{:S(2)}, u32[]{:S(2)}) %collective-permute-start.3) | collective-permute-done | bytes 524320 | tf_op jit(solution)/shard_map/ppermute | solution.py:22
  168.9 0.1 pad_maximum_fusion.2
  169.0 0.2 reverse_select_fusion.2
  169.2 3.7 collective-permute-start.4
  172.9 45.9 %collective-permute-done.4 = bf16[16,64,512]{2,1,0:T(8,128)(2,1)S(1)} collective-permute-done((bf16[16,64,512]{2,1,0:T(8,128)(2,1)S(1)}, bf16[16,64,512]{2,1,0:T(8,128)(2,1)S(1)}, u32[]{:S(2)}, u32[]{:S(2)}) %collective-permute-start.4) | collective-permute-done | bytes 1048608 | tf_op jit(solution)/shard_map/ppermute | solution.py:22
  218.8 0.2 pad_maximum_fusion.1
  219.0 0.6 reverse_select_fusion.1
  219.6 4.7 %collective-permute-start.5 = (bf16[32,64,512]{2,1,0:T(8,128)(2,1)S(1)}, bf16[32,64,512]{2,1,0:T(8,128)(2,1)}, u32[]{:S(2)}, u32[]{:S(2)}) collective-permute-start(bf16[32,64,512]{2,1,0:T(8,128)(2,1)S(1)} %bitcast.107), channel_id=1, source_target_pairs={{0,256},{8,264},{16,272},{24,280},{32,288},{40,296},{48,304},{56,3... | collective-permute-start | bytes 6291464 | tf_op jit(solution)/shard_map/ppermute | solution.py:22
  224.3 92.2 %collective-permute-done.5 = bf16[32,64,512]{2,1,0:T(8,128)(2,1)} collective-permute-done((bf16[32,64,512]{2,1,0:T(8,128)(2,1)S(1)}, bf16[32,64,512]{2,1,0:T(8,128)(2,1)}, u32[]{:S(2)}, u32[]{:S(2)}) %collective-permute-start.5) | collective-permute-done | bytes 2097184 | tf_op jit(solution)/shard_map/ppermute | solution.py:22
  316.6 2.0 pad_maximum_fusion
  318.6 1.2 reverse_select_fusion
  319.8 0.8 fusion.8
  320.7 20.4 %all_to_all.67 = bf16[8,64,512]{2,1,0:T(8,128)(2,1)S(1)} all-to-all(bf16[8,64,512]{2,1,0:T(8,128)(2,1)S(1)} %broadcast_in_dim.37), channel_id=1, replica_groups=mesh['row'=16,'col'=4,'depth'=8] {'depth'}, dimensions={0} | all-to-all | bytes 1048576 | tf_op jit(solution)/shard_map/all_to_all | solution.py:33
  341.1 0.8 fusion
  342.0 20.2 %all_to_all.68 = bf16[8,64,512]{2,1,0:T(8,128)(2,1)S(1)} all-to-all(bf16[8,64,512]{2,1,0:T(8,128)(2,1)S(1)} %broadcast_in_dim.38), channel_id=1, replica_groups=mesh['row'=16,'col'=4,'depth'=8] {'depth'}, dimensions={0} | all-to-all | bytes 1048576 | tf_op jit(solution)/shard_map/all_to_all | solution.py:33
  362.3 0.8 fusion.1
  363.1 19.3 %all_to_all.69 = bf16[8,64,512]{2,1,0:T(8,128)(2,1)S(1)} all-to-all(bf16[8,64,512]{2,1,0:T(8,128)(2,1)S(1)} %broadcast_in_dim.39), channel_id=1, replica_groups=mesh['row'=16,'col'=4,'depth'=8] {'depth'}, dimensions={0} | all-to-all | bytes 1048576 | tf_op jit(solution)/shard_map/all_to_all | solution.py:33
  382.4 0.8 fusion.2
  383.3 18.2 %all_to_all.70 = bf16[8,64,512]{2,1,0:T(8,128)(2,1)S(1)} all-to-all(bf16[8,64,512]{2,1,0:T(8,128)(2,1)S(1)} %broadcast_in_dim.40), channel_id=1, replica_groups=mesh['row'=16,'col'=4,'depth'=8] {'depth'}, dimensions={0} | all-to-all | bytes 1048576 | tf_op jit(solution)/shard_map/all_to_all | solution.py:33
  401.6 0.8 fusion.3
  402.5 17.6 %all_to_all.71 = bf16[8,64,512]{2,1,0:T(8,128)(2,1)S(1)} all-to-all(bf16[8,64,512]{2,1,0:T(8,128)(2,1)S(1)} %broadcast_in_dim.41), channel_id=1, replica_groups=mesh['row'=16,'col'=4,'depth'=8] {'depth'}, dimensions={0} | all-to-all | bytes 1048576 | tf_op jit(solution)/shard_map/all_to_all | solution.py:33
  420.2 0.8 fusion.4
  421.0 0.9 broadcast_in_dim.42
  421.9 3.5 all-to-all-start.9
  425.4 14.3 %all-to-all-done.9 = bf16[8,64,512]{2,1,0:T(8,128)(2,1)S(1)} async-done(((bf16[8,64,512]{2,1,0:T(8,128)(2,1)}), bf16[8,64,512]{2,1,0:T(8,128)(2,1)S(1)}, u32[]{:S(2)}, u32[]{:S(2)}) %all-to-all-start.9) | async-done | bytes 524320 | tf_op jit(solution)/shard_map/all_to_all | solution.py:33
  439.7 3.7 fusion.7
  (29 shorter events, 0.7 us)
Async XLA Ops:
  0.0 50.8 %copy-start.3 = (bf16[1,64,4096]{2,1,0:T(8,128)(2,1)S(1)}, bf16[1,64,4096]{2,1,0:T(8,128)(2,1)}, u32[]{:S(2)}) copy-start(bf16[1,64,4096]{2,1,0:T(8,128)(2,1)} %param.6) | copy-start | bytes 1572868
  0.0 50.8 %copy-start.2 = (bf16[1,64,4096]{2,1,0:T(8,128)(2,1)S(1)}, bf16[1,64,4096]{2,1,0:T(8,128)(2,1)}, u32[]{:S(2)}) copy-start(bf16[1,64,4096]{2,1,0:T(8,128)(2,1)} %param.5) | copy-start | bytes 1572868
  3.3 22.5 %all-to-all-start = ((bf16[64,1,2,64]{3,2,1,0:T(2,128)(2,1)}), bf16[64,1,2,64]{3,2,1,0:T(2,128)(2,1)S(1)}, u32[]{:S(2)}, u32[]{:S(2)}) async-start(bf16[64,1,2,64]{3,2,1,0:T(2,128)(2,1)} %broadcast_in_dim.35), calls=%async_computation | async-start | bytes 65536 | tf_op jit(solution)/shard_map/all_to_all | solution.py:33
  134.8 6.2 %collective-permute-start = (bf16[1,64,512]{2,1,0:T(8,128)(2,1)S(1)}, bf16[1,64,512]{2,1,0:T(8,128)(2,1)S(1)}, u32[]{:S(2)}, u32[]{:S(2)}) collective-permute-start(bf16[1,64,512]{2,1,0:T(8,128)(2,1)S(1)} %get-tuple-element.10), channel_id=1, source_target_pairs={{0,8},{8,0},{16,24},{24,16},{32,40},{40,32},{48,56},{56,48},{64,72... | collective-permute-start | bytes 196616 | tf_op jit(solution)/shard_map/ppermute | solution.py:22
  141.0 8.4 %collective-permute-start.1 = (bf16[2,64,512]{2,1,0:T(8,128)(2,1)S(1)}, bf16[2,64,512]{2,1,0:T(8,128)(2,1)S(1)}, u32[]{:S(2)}, u32[]{:S(2)}) collective-permute-start(bf16[2,64,512]{2,1,0:T(8,128)(2,1)S(1)} %get-tuple-element.8), channel_id=1, source_target_pairs={{0,16},{8,24},{16,0},{24,8},{32,48},{40,56},{48,32},{56,40},{64,80... | collective-permute-start | bytes 393224 | tf_op jit(solution)/shard_map/ppermute | solution.py:22
  149.5 3.4 collective-permute-start.2
  153.1 15.9 %collective-permute-start.3 = (bf16[8,64,512]{2,1,0:T(8,128)(2,1)S(1)}, bf16[8,64,512]{2,1,0:T(8,128)(2,1)S(1)}, u32[]{:S(2)}, u32[]{:S(2)}) collective-permute-start(bf16[8,64,512]{2,1,0:T(8,128)(2,1)S(1)} %bitcast.124), channel_id=1, source_target_pairs={{0,64},{8,72},{16,80},{24,88},{32,96},{40,104},{48,112},{56,120},{... | collective-permute-start | bytes 1572872 | tf_op jit(solution)/shard_map/ppermute | solution.py:22
  169.2 49.6 %collective-permute-start.4 = (bf16[16,64,512]{2,1,0:T(8,128)(2,1)S(1)}, bf16[16,64,512]{2,1,0:T(8,128)(2,1)S(1)}, u32[]{:S(2)}, u32[]{:S(2)}) collective-permute-start(bf16[16,64,512]{2,1,0:T(8,128)(2,1)S(1)} %bitcast.111), channel_id=1, source_target_pairs={{0,128},{8,136},{16,144},{24,152},{32,160},{40,168},{48,176},{56,1... | collective-permute-start | bytes 3145736 | tf_op jit(solution)/shard_map/ppermute | solution.py:22
  219.6 97.0 %collective-permute-start.5 = (bf16[32,64,512]{2,1,0:T(8,128)(2,1)S(1)}, bf16[32,64,512]{2,1,0:T(8,128)(2,1)}, u32[]{:S(2)}, u32[]{:S(2)}) collective-permute-start(bf16[32,64,512]{2,1,0:T(8,128)(2,1)S(1)} %bitcast.107), channel_id=1, source_target_pairs={{0,256},{8,264},{16,272},{24,280},{32,288},{40,296},{48,304},{56,3... | collective-permute-start | bytes 6291464 | tf_op jit(solution)/shard_map/ppermute | solution.py:22
  318.6 1.2 copy-start.1
  319.8 100.4 %copy-start = (bf16[2,32,64,512]{3,2,1,0:T(8,128)(2,1)}, bf16[2,32,64,512]{3,2,1,0:T(8,128)(2,1)S(1)}, u32[]{:S(2)}) copy-start(bf16[2,32,64,512]{3,2,1,0:T(8,128)(2,1)S(1)} %reverse_select_fusion) | copy-start | bytes 12582916
  421.9 17.8 %all-to-all-start.9 = ((bf16[8,64,512]{2,1,0:T(8,128)(2,1)}), bf16[8,64,512]{2,1,0:T(8,128)(2,1)S(1)}, u32[]{:S(2)}, u32[]{:S(2)}) async-start(bf16[8,64,512]{2,1,0:T(8,128)(2,1)} %broadcast_in_dim.42), calls=%async_computation.9 | async-start | bytes 1048576 | tf_op jit(solution)/shard_map/all_to_all | solution.py:33
